TPU v7x, 32 devices: a whole 2x2x4 slice. The times are simulated.
32 devices in a mesh: group: 2 (over y), seq: 4 (over x, core), dom: 4 (over z).
Axes of the slice: x: 2, y: 2, z: 4, core: 2. Of those that a mesh axis runs over, the one named last changes fastest.
Arguments:
- q_nope: bfloat16 [32, 128, 128], P(('group', 'dom'), 'seq'), parts along dimension 0, may hold values from -6 to 6
- q_rope: bfloat16 [32, 128, 64], P(('group', 'dom'), 'seq'), parts along dimension 0, may hold values from -8 to 8
- w_uk: bfloat16 [128, 128, 512], P('seq'), may hold values from -0.5 to 0.5
- w_uv: bfloat16 [128, 512, 128], P('seq'), may hold values from -1.5 to 1.5
- prefix: bfloat16 [32768, 576], P(('group', 'seq')), parts along dimension 0, may hold values from -8 to 8
- private_caches: bfloat16 [32, 256, 576], P(('group', 'dom'), 'seq'), parts along dimension 0, may hold values from -8 to 8
- new_latent: bfloat16 [32, 576], P(('group', 'dom')), parts along dimension 0, may hold values from -6 to 6
- ancestors: int32 [32], P(('group', 'dom')), parts along dimension 0, may hold values from 0 to 15
- lengths: int32 [32], P('group'), parts along dimension 0, may hold values from 1 to 255
Outputs:
- head_values: bfloat16 [32, 128, 128], P(('group', 'dom'), 'seq'), parts along dimension 0
- new_caches: bfloat16 [32, 256, 576], P(('group', 'dom'), 'seq'), parts along dimension 0
There are 2 independent parts, one for each index of `group`. A program takes and returns all parts, laid end to end along the dimension named above; an argument that names none is the same for every part. Nothing has to cross between parts.
All inputs are finite; a program needn't handle non-finite values.
Results may differ from a plain program's by a relative error of at most 0.0085.
Values may be sent and summed in bfloat16 or wider, within the bound.
A program may use at most 64 MiB of HBM per device.

v0:
```python
import jax
import jax.numpy as jnp
from jax import lax
from jax.sharding import PartitionSpec as P

ROPE = 64
NOPE = 128


masked_score = -1e30


def joined(part, axis, combine):
    gathered = jax.tree.map(lambda a: lax.all_gather(a, axis), part)

    def take(source):
        return jax.tree.map(lambda a: lax.dynamic_index_in_dim(a, source, 0, False), gathered)

    return lax.fori_loop(
        1, lax.axis_size(axis), lambda source, state: combine(state, take(source)), take(0)
    )


def merge_partials(left_part, right_part):
    left_max, left_sum, left_acc = left_part
    right_max, right_sum, right_acc = right_part
    largest = jnp.maximum(left_max, right_max)
    left_factor = jnp.exp(left_max - largest)
    right_factor = jnp.exp(right_max - largest)
    return (
        largest,
        left_sum * left_factor + right_sum * right_factor,
        left_acc * left_factor[..., None] + right_acc * right_factor[..., None],
    )


def on_device(q_nope, q_rope, w_uk, w_uv, prefix, private_caches, new_latent, ancestors, lengths):
    softmax_scale = (NOPE + ROPE) ** (-0.5)
    local_count = ancestors.shape[0]
    particle_total = lengths.shape[0]
    suffix_rows = private_caches.shape[1]
    latent_width = private_caches.shape[2]
    latent_rank = w_uv.shape[1]
    own_heads = w_uv.shape[0]
    seq_index = lax.axis_index("seq")
    portion = lax.all_gather(private_caches, "dom", axis=0, tiled=True)
    amount = portion.shape[0]
    picks = (ancestors[:, None] == jnp.arange(amount, dtype=jnp.int32)[None, :]).astype(
        jnp.bfloat16
    )
    gathered = jnp.dot(picks, portion.reshape(amount, -1), preferred_element_type=jnp.float32)
    migrated = gathered.astype(jnp.bfloat16).reshape(local_count, suffix_rows, latent_width)
    owners = ancestors[:, None] == jnp.arange(particle_total, dtype=jnp.int32)[None, :]
    new_lengths = jnp.sum(jnp.where(owners, lengths[None, :], 0), axis=1)
    positions = seq_index * suffix_rows + jnp.arange(suffix_rows, dtype=jnp.int32)
    writes = positions[None, :] == new_lengths[:, None]
    new_caches = jnp.where(writes[:, :, None], new_latent[:, None, :], migrated)
    query_latent = jnp.einsum(
        "phn,hnc->phc", q_nope, w_uk, preferred_element_type=jnp.float32
    ).astype(jnp.bfloat16)
    own_queries = jnp.concatenate([query_latent, q_rope], axis=2)
    all_queries = lax.all_gather(own_queries, "seq", axis=1, tiled=True)
    head_total = all_queries.shape[1]
    flat_queries = all_queries.reshape(local_count * head_total, latent_width)
    prefix_scores = (
        lax.dot_general(
            flat_queries, prefix, (((1,), (1,)), ((), ())), preferred_element_type=jnp.float32
        )
        * softmax_scale
    )
    prefix_max = jnp.max(prefix_scores, axis=1)
    prefix_weights = jnp.exp(prefix_scores - prefix_max[:, None])
    prefix_sum = jnp.sum(prefix_weights, axis=1)
    prefix_acc = jnp.dot(
        prefix_weights.astype(jnp.bfloat16),
        prefix[:, :latent_rank],
        preferred_element_type=jnp.float32,
    )
    prefix_part = (
        prefix_max.reshape(local_count, head_total),
        prefix_sum.reshape(local_count, head_total),
        prefix_acc.reshape(local_count, head_total, latent_rank),
    )
    suffix_scores = (
        jnp.einsum("phc,pkc->phk", all_queries, migrated, preferred_element_type=jnp.float32)
        * softmax_scale
    )
    visible = (positions[None, :] < new_lengths[:, None])[:, None, :]
    masked = jnp.where(visible, suffix_scores, masked_score)
    suffix_max = jnp.max(masked, axis=2)
    suffix_weights = jnp.where(visible, jnp.exp(masked - suffix_max[:, :, None]), 0.0)
    suffix_sum = jnp.sum(suffix_weights, axis=2)
    suffix_acc = jnp.einsum(
        "phk,pkc->phc",
        suffix_weights.astype(jnp.bfloat16),
        migrated[:, :, :latent_rank],
        preferred_element_type=jnp.float32,
    )
    local_part = merge_partials(prefix_part, (suffix_max, suffix_sum, suffix_acc))
    merged = joined(local_part, "seq", merge_partials)
    first_head = seq_index * own_heads
    denominator = lax.dynamic_slice_in_dim(merged[1], first_head, own_heads, 1)
    numerator = lax.dynamic_slice_in_dim(merged[2], first_head, own_heads, 1)
    latent_out = (numerator / denominator[:, :, None]).astype(jnp.bfloat16)
    head_values = jnp.einsum(
        "phc,hcv->phv", latent_out, w_uv, preferred_element_type=jnp.float32
    ).astype(jnp.bfloat16)
    return (head_values, new_caches)


def solution(mesh):
    placed = (
        P(("group", "dom"), "seq", None),
        P(("group", "dom"), "seq", None),
        P("seq", None, None),
        P("seq", None, None),
        P(("group", "seq"), None),
        P(("group", "dom"), "seq", None),
        P(("group", "dom"), None),
        P(("group", "dom")),
        P("group"),
    )
    return jax.shard_map(
        on_device,
        mesh=mesh,
        in_specs=placed,
        out_specs=(P(("group", "dom"), "seq", None), P(("group", "dom"), "seq", None)),
        check_vma=False,
    )
```

profile of v0, /device:TPU:0, one launch (start us, length us, event | category | flops | bytes accessed | tf_op | source)
XLA Modules:
  0.0 100.5 jit_solution(9597892583069278316)
XLA Ops:
  7.2 0.7 all-gather.4.cloned.1.call-update
  8.0 0.8 copy.29
  8.8 2.8 %fusion.12 = bf16[4,32,512]{2,0,1:T(4,128)(2,1)S(1)} fusion(bf16[32,128,512]{2,1,0:T(8,128)(2,1)} %param.13, bf16[4,32,128]{2,1,0:T(8,128)(2,1)S(1)} %copy-done), kind=kOutput, calls=%fused_computation.22 | convolution fusion | flops 16842752 | bytes 4358144 | tf_op jit(solution)/shard_map/phn,hnc->phc/dot_general | solution.py:58
  11.7 9.4 %all_gather.20 = bf16[4,128,576]{2,0,1:T(4,128)(2,1)S(1)} all-gather(bf16[4,32,576]{2,0,1:T(4,128)(2,1)S(1)} %pad_maximum_fusion), channel_id=1, replica_groups=mesh['group'=2,'seq'=4,'dom'=4] {'seq'}, dimensions={1}, use_global_device_ids=true | all-gather | bytes 737280 | tf_op jit(solution)/shard_map/all_gather | solution.py:62
  21.1 0.9 copy.30
  22.3 5.7 %multiply_reduce_fusion = (f32[512]{0:T(512)S(1)}, f32[512,4096]{1,0:T(8,128)S(1)}) fusion(bf16[4096,576]{0,1:T(8,128)(2,1)} %param.15, bf16[72,8,4,128]{3,2,1,0:T(4,128)(2,1)S(1)} %bitcast.74), kind=kOutput, calls=%fused_computation.10 | convolution fusion | flops 2420112896 | bytes 13699072 | tf_op jit(solution)/shard_map/dot_general | solution.py:66
  28.0 3.2 %copy-done.1 = f32[512,4096]{1,0:T(8,128)} copy-done((f32[512,4096]{1,0:T(8,128)}, f32[512,4096]{1,0:T(8,128)S(1)}, u32[]{:S(2)}) %copy-start.1) | copy-done | bytes 8388632
  31.3 2.5 %fusion.5 = f32[512,512]{1,0:T(8,128)S(1)} fusion(f32[512,4096]{1,0:T(8,128)S(1)} %get-tuple-element.216, bf16[4096,576]{0,1:T(8,128)(2,1)S(1)} %bitcast.73, f32[512]{0:T(512)S(1)} %get-tuple-element.215), kind=kOutput, calls=%fused_computation.13 | convolution fusion | flops 2153775104 | bytes 13633536 | tf_op jit(solution)/shard_map/dot_general | solution.py:74
  33.7 11.1 %all-gather.4.cloned.1.call-done = bf16[16,64,576]{2,1,0:T(8,128)(2,1)} async-done(((bf16[4,64,576]{2,1,0:T(8,128)(2,1)}), bf16[16,64,576]{2,1,0:T(8,128)(2,1)}) %all-gather.4.cloned.1.call-update) | async-done | bytes 1179664 | tf_op jit(solution)/shard_map/all_gather | solution.py:46
  44.9 2.7 %reshape.166 = bf16[16,36864]{1,0:T(8,128)(2,1)S(1)} reshape(bf16[16,64,576]{2,1,0:T(8,128)(2,1)} %all-gather.4.cloned.1.call-done) | data formatting | bytes 2359296 | tf_op jit(solution)/shard_map/reshape | solution.py:51
  48.3 0.4 fusion.36
  48.7 1.5 %fusion.10 = f32[4,128,512]{2,1,0:T(8,128)} fusion(f32[4,128,512]{2,1,0:T(8,128)S(1)} %bitcast.75, f32[4,128]{1,0:T(4,128)S(1)} %get-tuple-element.208, f32[4,128]{1,0:T(4,128)S(1)} %get-tuple-element.207, bf16[4,64,576]{2,1,0:T(8,128)(2,1)S(1)} %reshape.167, f32[4,128,64]{1,2,0:T(8,128)S(1)} %get-tuple-element.214, f32[4,128]{1,0:T(4,128)S(1)} %get-tuple-element.213, ...), kind=kOutput, calls=%fused_computation.18 | convolution fusion | flops 34439168 | bytes 2497024 | tf_op jit(solution)/shard_map/phk,pkc->phc/dot_general | solution.py:93
  50.2 4.9 %fusion.4 = f32[512]{0:T(512)S(1)} fusion(f32[512,4096]{1,0:T(8,128)} %copy-done.1, f32[512]{0:T(512)S(1)} %get-tuple-element.215), kind=kLoop, calls=%fused_computation.12 | loop fusion | flops 6290944 | bytes 8392704 | tf_op jit(solution)/shard_map/reduce_sum | solution.py:73
  55.2 5.2 %all_gather.22 = f32[4,4,128]{2,1,0:T(4,128)S(1)} all-gather(f32[1,4,128]{2,1,0:T(4,128)S(1)} %get-tuple-element.210), channel_id=1, replica_groups=mesh['group'=2,'seq'=4,'dom'=4] {'seq'}, dimensions={0}, use_global_device_ids=true | all-gather | bytes 10240 | tf_op jit(solution)/shard_map/all_gather | solution.py:14
  60.4 5.3 %all_gather.23 = f32[4,4,128]{2,1,0:T(4,128)S(1)} all-gather(f32[1,4,128]{2,1,0:T(4,128)S(1)} %get-tuple-element.209), channel_id=1, replica_groups=mesh['group'=2,'seq'=4,'dom'=4] {'seq'}, dimensions={0}, use_global_device_ids=true | all-gather | bytes 10240 | tf_op jit(solution)/shard_map/all_gather | solution.py:14
  65.8 0.8 broadcast_select_fusion
  66.6 17.4 %all-gather.6.cloned.1.call-done = f32[16,128,512]{2,1,0:T(8,128)} async-done(((f32[4,128,512]{2,1,0:T(8,128)}), f32[16,128,512]{2,1,0:T(8,128)}) %all-gather.6.cloned.1.call-update) | async-done | bytes 4194320 | tf_op jit(solution)/shard_map/all_gather | solution.py:14
  84.0 1.3 %slice.13 = f32[4,128,512]{2,1,0:T(8,128)S(1)} slice(f32[16,128,512]{2,1,0:T(8,128)} %all-gather.6.cloned.1.call-done), slice={[0:4], [0:128], [0:512]} | slice | bytes 2097152 | tf_op jit(solution)/shard_map/jit(dynamic_index_in_dim)/dynamic_slice | solution.py:17
  85.3 4.7 %while.19 = (s32[]{:T(128)}, f32[4,128]{1,0:T(4,128)S(1)}, f32[4,128]{1,0:T(4,128)S(1)}, f32[4,128,512]{2,1,0:T(8,128)S(1)}, f32[4,4,128]{2,1,0:T(4,128)S(1)}, /...) while((s32[]{:T(128)}, f32[4,128]{1,0:T(4,128)S(1)}, ...), condition=%wide.region_6.7_spmd, body=%wide.region_5.6_spmd.sunk | while | flops 789509 | bytes 3166359 | solution.py:19
  85.3 1.5 %fusion.45 = f32[4,128,512]{2,1,0:T(8,128)S(1)} fusion(f32[4,4,128,512]{3,2,1,0:T(8,128)} %get-tuple-element.294, s32[]{:T(128)S(6)} %select_n.51, f32[4,128,512]{2,1,0:T(8,128)S(1)} %get-tuple-element.281, f32[4,128]{1,0:T(4,128)S(1)} %get-tuple-element.266, f32[4,128]{1,0:T(4,128)S(1)} %get-tuple-element.267), kind=kLoop, calls=%fused_computation.1.clone.1 | loop fusion | flops 786432 | bytes 3149828 | tf_op jit(solution)/shard_map/while/body/eval_jaxpr/add | solution.py:33
  86.9 1.5 %fusion.45 = f32[4,128,512]{2,1,0:T(8,128)S(1)} fusion(f32[4,4,128,512]{3,2,1,0:T(8,128)} %get-tuple-element.294, s32[]{:T(128)S(6)} %select_n.51, f32[4,128,512]{2,1,0:T(8,128)S(1)} %get-tuple-element.281, f32[4,128]{1,0:T(4,128)S(1)} %get-tuple-element.266, f32[4,128]{1,0:T(4,128)S(1)} %get-tuple-element.267), kind=kLoop, calls=%fused_computation.1.clone.1 | loop fusion | flops 786432 | bytes 3149828 | tf_op jit(solution)/shard_map/while/body/eval_jaxpr/add | solution.py:33
  88.5 1.5 %fusion.45 = f32[4,128,512]{2,1,0:T(8,128)S(1)} fusion(f32[4,4,128,512]{3,2,1,0:T(8,128)} %get-tuple-element.294, s32[]{:T(128)S(6)} %select_n.51, f32[4,128,512]{2,1,0:T(8,128)S(1)} %get-tuple-element.281, f32[4,128]{1,0:T(4,128)S(1)} %get-tuple-element.266, f32[4,128]{1,0:T(4,128)S(1)} %get-tuple-element.267), kind=kLoop, calls=%fused_computation.1.clone.1 | loop fusion | flops 786432 | bytes 3149828 | tf_op jit(solution)/shard_map/while/body/eval_jaxpr/add | solution.py:33
  90.2 2.8 %fusion.13 = bf16[4,32,128]{2,0,1:T(4,128)(2,1)S(1)} fusion(bf16[32,512,128]{2,1,0:T(8,128)(2,1)} %param.14, bf16[4,32,512]{2,1,0:T(8,128)(2,1)S(1)} %divide_convert_fusion), kind=kOutput, calls=%fused_computation.24 | convolution fusion | flops 16793600 | bytes 4358144 | tf_op jit(solution)/shard_map/phc,hcv->phv/dot_general | solution.py:105
  93.0 0.6 copy.33
  (33 shorter events, 1.6 us)
Async XLA Ops:
  7.2 1.6 %copy-start = (bf16[4,32,128]{2,1,0:T(8,128)(2,1)S(1)}, bf16[4,32,128]{2,1,0:T(8,128)(2,1)}, u32[]{:S(2)}) copy-start(bf16[4,32,128]{2,1,0:T(8,128)(2,1)} %param.11) | copy-start | bytes 98308
  7.2 14.8 %copy-start.3 = (s32[4]{0:T(128)S(1)}, s32[4]{0:T(128)}, u32[]{:S(2)}) copy-start(s32[4]{0:T(128)} %param.18) | copy-start | bytes 52
  7.2 14.8 %copy-start.4 = (s32[16]{0:T(128)S(1)}, s32[16]{0:T(128)}, u32[]{:S(2)}) copy-start(s32[16]{0:T(128)} %param.19) | copy-start | bytes 196
  7.2 37.7 %all-gather.4.cloned.1.call-start = ((), (), s32[]{:S(2)}) async-start(), calls=%async_computation | async-start | bytes 1638400 | tf_op jit(solution)/shard_map/all_gather | solution.py:46
  7.9 76.0 %all-gather.6.cloned.1.call-start = ((), (), s32[]{:S(2)}) async-start(), calls=%async_computation.1 | async-start | bytes 5242880 | tf_op jit(solution)/shard_map/all_gather | solution.py:14
  21.1 10.2 %slice-start = ((s8[4718592]{0:T(1024)(128)(4,1)}), s8[524288]{0:T(1024)(128)(4,1)S(1)}, s32[]{:S(2)}) async-start(s8[4718592]{0:T(1024)(128)(4,1)} %bitcast.72), calls=%async_computation.2 | async-start | bytes 1048576
  22.3 9.0 %slice-start.1 = ((s8[4718592]{0:T(1024)(128)(4,1)}), s8[4194304]{0:T(1024)(128)(4,1)S(1)}, s32[]{:S(2)}) async-start(s8[4718592]{0:T(1024)(128)(4,1)} %bitcast.72), calls=%async_computation.3 | async-start | bytes 8388608
  28.0 3.2 %copy-start.1 = (f32[512,4096]{1,0:T(8,128)}, f32[512,4096]{1,0:T(8,128)S(1)}, u32[]{:S(2)}) copy-start(f32[512,4096]{1,0:T(8,128)S(1)} %get-tuple-element.216) | copy-start | bytes 25165828
  50.2 15.6 %copy-start.2 = (bf16[4,576]{1,0:T(4,128)(2,1)S(1)}, bf16[4,576]{1,0:T(4,128)(2,1)}, u32[]{:S(2)}) copy-start(bf16[4,576]{1,0:T(4,128)(2,1)} %param.17) | copy-start | bytes 13828
Sparse Core Ops, SparseCore 0:
  9.6 35.2 all-gather.3
  50.3 33.5 all-gather.5
where the time goes:
time: 101 us
  waiting for transfers between devices  29.2 us (29%)
  blocking collectives  19.9 us (20%)
  matrix products  16.1 us (16%)
  between operations  14.2 us (14%)
  other arithmetic  11 us (11%)
  local copies, waits for them, and re-layouts  10 us (10%)
    all_gather x1, waiting for transfers between devices, joined(): gathered = jax.tree.map(lambda a: lax.all_gather(a, axis), part)  17.4 us
    all_gather x1, waiting for transfers between devices, on_device(): portion = lax.all_gather(private_caches, 'dom', axis=0, tiled=True)  11.1 us
    all_gather x2, blocking collectives, joined(): gathered = jax.tree.map(lambda a: lax.all_gather(a, axis), part)  10.5 us
    all_gather x1, blocking collectives, on_device(): all_queries = lax.all_gather(own_queries, 'seq', axis=1, tiled=True)  9.36 us
    dot_general x1, matrix products, on_device(): lax.dot_general(flat_queries, prefix, (((1,), (1,)), ((), ())), preferred...  5.71 us
    reduce_sum x1, other arithmetic, on_device(): prefix_sum = jnp.sum(prefix_weights, axis=1)  4.88 us
    unnamed x16, local copies, waits for them, and re-layouts  4.67 us
    add x3, other arithmetic, merge_partials(): left_acc * left_factor[..., None] + right_acc * right_factor[..., None]  4.56 us
  transfers between devices with their start and end apart: 2, of which 2 were waited for; matrix products, arithmetic and copies ran while one was open for 19% of the time, Pallas kernels for 0%

commit v1 on v0

v1 whole, which is shorter than its diff:
```python
import functools

import jax
import jax.numpy as jnp
from jax import lax
from jax.experimental import pallas as pl
from jax.experimental.pallas import tpu as pltpu
from jax.sharding import PartitionSpec as P

ROPE = 64
NOPE = 128

MASKED = -1e30
KEY_TILE = 512


def partner(index, step, count):
    if count & (count - 1):
        raise ValueError("seq size")
    other = index
    bit = 1
    while bit <= step:
        if step & bit:
            other = other + bit - 2 * bit * lax.rem(index // bit, 2)
        bit *= 2
    return other


def attention_kernel(
    n_seq, n_dom, scale,
    anc_ref, len_ref, q_ref, prefix_hbm, cache_ref, fresh_ref,
    latent_ref, caches_ref,
    queries, prefix, blocks, suffix, scores, acc, stats,
    send_acc, send_stat, recv_acc, recv_stat,
    load_sem, q_send, q_recv, z_send, z_recv, a_send, a_recv, s_send, s_recv,
):
    me = lax.axis_index("seq")
    dom = lax.axis_index("dom")
    local = cache_ref.shape[0]
    rows_suffix = cache_ref.shape[1]
    width = cache_ref.shape[2]
    rows = q_ref.shape[0]
    heads = rows // local
    rank = latent_ref.shape[1]
    keys = prefix.shape[0]
    group = 2 if n_seq % 2 == 0 else 1

    load = pltpu.make_async_copy(prefix_hbm, prefix, load_sem)
    load.start()

    barrier = pltpu.get_barrier_semaphore()
    for step in range(1, n_seq):
        pl.semaphore_signal(barrier, inc=1, device_id={"seq": partner(me, step, n_seq)})

    @pl.when(dom > 0)
    def _():
        pl.semaphore_signal(barrier, inc=1, device_id={"dom": dom - 1})

    @pl.when(dom < n_dom - 1)
    def _():
        pl.semaphore_signal(barrier, inc=1, device_id={"dom": dom + 1})

    below = lax.div(dom + n_dom - 1, n_dom)
    above = lax.div(2 * n_dom - 2 - dom, n_dom)
    pl.semaphore_wait(barrier, n_seq - 1 + below + above)

    def q_copy(step):
        return pltpu.make_async_remote_copy(
            src_ref=q_ref, dst_ref=queries.at[step],
            send_sem=q_send.at[step], recv_sem=q_recv.at[step],
            device_id={"seq": partner(me, step, n_seq)},
        )

    def z_copy(way, step):
        block = dom - step if way == 0 else dom + step
        view = blocks.at[pl.ds(block * local, local)]
        return pltpu.make_async_remote_copy(
            src_ref=cache_ref if step == 0 else view, dst_ref=view,
            send_sem=z_send.at[way, step], recv_sem=z_recv.at[way, step],
            device_id={"dom": dom + 1 if way == 0 else dom - 1},
        )

    def z_arrival(way, step):
        block = dom - step - 1 if way == 0 else dom + step + 1
        view = blocks.at[pl.ds(block * local, local)]
        return pltpu.make_async_remote_copy(
            src_ref=view, dst_ref=view,
            send_sem=z_send.at[way, step], recv_sem=z_recv.at[way, step],
            device_id={"dom": dom + 1 if way == 0 else dom - 1},
        )

    def z_sends(way, step):
        if way == 0:
            return (dom >= step) & (dom < n_dom - 1)
        return (dom + step < n_dom) & (dom > 0)

    def z_receives(way, step):
        if way == 0:
            return dom >= step + 1
        return dom + step + 1 < n_dom

    def z_stage(step):
        for way in (0, 1):
            if step > 0:
                @pl.when(z_receives(way, step - 1))
                def _():
                    z_arrival(way, step - 1).wait_recv()
            if step < n_dom - 1:
                @pl.when(z_sends(way, step))
                def _():
                    z_copy(way, step).start()

    for step in range(1, n_seq):
        q_copy(step).start()
    z_stage(0)
    queries[0] = q_ref[...]
    blocks[pl.ds(dom * local, local)] = cache_ref[...]
    load.wait()
    stage = 1

    for first in range(0, n_seq, group):
        for step in range(max(first, 1), first + group):
            q_copy(step).wait_recv()
        wide = group * rows
        flat = queries[first : first + group].reshape(wide, width)
        peak = jnp.full((wide, 128), MASKED, jnp.float32)
        for tile in range(keys // KEY_TILE):
            part = lax.dot_general(
                flat, prefix[tile * KEY_TILE : (tile + 1) * KEY_TILE],
                (((1,), (1,)), ((), ())), preferred_element_type=jnp.float32,
            ) * scale
            scores[:, tile * KEY_TILE : (tile + 1) * KEY_TILE] = part
            for lane in range(KEY_TILE // 128):
                peak = jnp.maximum(peak, part[:, lane * 128 : (lane + 1) * 128])
        top = jnp.max(peak, axis=1, keepdims=True)
        mass = jnp.zeros((wide, 128), jnp.float32)
        for tile in range(keys // KEY_TILE):
            weights = jnp.exp(scores[:, tile * KEY_TILE : (tile + 1) * KEY_TILE] - top)
            for lane in range(KEY_TILE // 128):
                mass = mass + weights[:, lane * 128 : (lane + 1) * 128]
            update = jnp.dot(
                weights.astype(jnp.bfloat16),
                prefix[tile * KEY_TILE : (tile + 1) * KEY_TILE, :rank],
                preferred_element_type=jnp.float32,
            )
            here = pl.ds(first * rows, wide)
            if tile == 0:
                acc[here] = update
            else:
                acc[here] += update
        total = jnp.sum(mass, axis=1, keepdims=True)
        stats[0, pl.ds(first * rows, wide)] = jnp.broadcast_to(top, (wide, 128))
        stats[1, pl.ds(first * rows, wide)] = jnp.broadcast_to(total, (wide, 128))
        if stage < n_dom:
            z_stage(stage)
            stage += 1
    while stage < n_dom:
        z_stage(stage)
        stage += 1

    place = me * rows_suffix + lax.broadcasted_iota(jnp.int32, (rows_suffix, width), 0)
    for p in range(local):
        source = anc_ref[p]
        length = len_ref[source]
        moved = blocks[source]
        suffix[p * rows_suffix : (p + 1) * rows_suffix] = moved
        fresh = jnp.broadcast_to(fresh_ref[p : p + 1].astype(jnp.float32), (rows_suffix, width))
        caches_ref[p] = jnp.where(place == length, fresh, moved.astype(jnp.float32)).astype(
            caches_ref.dtype
        )

    span = local * rows_suffix
    wide = group * rows
    row_p = lax.rem(lax.broadcasted_iota(jnp.int32, (wide, span), 0), rows) // heads
    column = lax.broadcasted_iota(jnp.int32, (wide, span), 1)
    visible = jnp.zeros((wide, span), jnp.bool_)
    for p in range(local):
        limit = jnp.clip(len_ref[anc_ref[p]] - me * rows_suffix, 0, rows_suffix)
        visible = visible | (
            (row_p == p) & (column >= p * rows_suffix) & (column < p * rows_suffix + limit)
        )

    def a_copy(step):
        return pltpu.make_async_remote_copy(
            src_ref=send_acc.at[step], dst_ref=recv_acc.at[step],
            send_sem=a_send.at[step], recv_sem=a_recv.at[step],
            device_id={"seq": partner(me, step, n_seq)},
        )

    def s_copy(step):
        return pltpu.make_async_remote_copy(
            src_ref=send_stat.at[step], dst_ref=recv_stat.at[step],
            send_sem=s_send.at[step], recv_sem=s_recv.at[step],
            device_id={"seq": partner(me, step, n_seq)},
        )

    lane = lax.broadcasted_iota(jnp.int32, (rows, 128), 1)
    for first in range(n_seq - group, -1, -group):
        here = pl.ds(first * rows, wide)
        flat = queries[first : first + group].reshape(wide, width)
        raw = lax.dot_general(
            flat, suffix[...], (((1,), (1,)), ((), ())), preferred_element_type=jnp.float32
        ) * scale
        masked = jnp.where(visible, raw, MASKED)
        old_top = stats[0, here][:, :1]
        top = jnp.maximum(old_top, jnp.max(masked, axis=1, keepdims=True))
        keep = jnp.exp(old_top - top)
        weights = jnp.where(visible, jnp.exp(masked - top), 0.0)
        total = stats[1, here][:, :1] * keep + jnp.sum(weights, axis=1, keepdims=True)
        final = acc[here] * keep + jnp.dot(
            weights.astype(jnp.bfloat16), suffix[:, :rank], preferred_element_type=jnp.float32
        )
        for offset in range(group - 1, -1, -1):
            step = first + offset
            mine = slice(offset * rows, (offset + 1) * rows)
            if step == 0:
                acc[pl.ds(0, rows)] = final[mine]
                stats[0, pl.ds(0, rows)] = jnp.broadcast_to(top[mine], (rows, 128))
                stats[1, pl.ds(0, rows)] = jnp.broadcast_to(total[mine], (rows, 128))
            else:
                send_acc[step] = final[mine].astype(jnp.bfloat16)
                packed = jnp.where(lane == 0, top[mine], total[mine])
                send_stat[step] = packed.T[:8, :]
                s_copy(step).start()
                a_copy(step).start()

    tops = [stats[0, pl.ds(0, rows)][:, :1]]
    totals = [stats[1, pl.ds(0, rows)][:, :1]]
    for step in range(1, n_seq):
        s_copy(step).wait_recv()
        got = jnp.concatenate(
            [recv_stat[step], jnp.zeros((120, rows), jnp.float32)], axis=0
        ).T
        tops.append(got[:, 0:1])
        totals.append(got[:, 1:2])
    largest = functools.reduce(jnp.maximum, tops)
    factors = [jnp.exp(t - largest) for t in tops]
    denominator = functools.reduce(jnp.add, [f * t for f, t in zip(factors, totals)])
    inverse = 1.0 / denominator
    result = acc[pl.ds(0, rows)] * (factors[0] * inverse)
    for step in range(1, n_seq):
        a_copy(step).wait_recv()
        result = result + recv_acc[step].astype(jnp.float32) * (factors[step] * inverse)
    latent_ref[...] = result.astype(latent_ref.dtype)

    for step in range(1, n_seq):
        q_copy(step).wait_send()
        a_copy(step).wait_send()
        s_copy(step).wait_send()
    for way in (0, 1):
        for step in range(n_dom - 1):
            @pl.when(z_sends(way, step))
            def _():
                z_copy(way, step).wait_send()


def on_device(
    n_seq, n_dom, q_nope, q_rope, w_uk, w_uv, prefix, private_caches, new_latent, ancestors, lengths
):
    scale = (NOPE + ROPE) ** (-0.5)
    local = ancestors.shape[0]
    rows_suffix, width = private_caches.shape[1:]
    own_heads, rank = w_uv.shape[:2]
    rows = local * own_heads
    padded = -(-rows // 128) * 128
    query_latent = jnp.einsum(
        "phn,hnc->phc", q_nope, w_uk, preferred_element_type=jnp.float32
    ).astype(jnp.bfloat16)
    own = jnp.concatenate([query_latent, q_rope], axis=2)
    if padded != rows:
        extra = padded // local - own_heads
        own = jnp.pad(own, ((0, 0), (0, extra), (0, 0)))
    own = own.reshape(padded, width)
    group = 2 if n_seq % 2 == 0 else 1
    vmem = pl.BlockSpec(memory_space=pltpu.VMEM)
    smem = pl.BlockSpec(memory_space=pltpu.SMEM)
    latent, new_caches = pl.pallas_call(
        functools.partial(attention_kernel, n_seq, n_dom, scale),
        out_shape=(
            jax.ShapeDtypeStruct((padded, rank), jnp.bfloat16),
            jax.ShapeDtypeStruct(private_caches.shape, jnp.bfloat16),
        ),
        in_specs=[smem, smem, vmem, pl.BlockSpec(memory_space=pl.ANY), vmem, vmem],
        out_specs=(vmem, vmem),
        scratch_shapes=[
            pltpu.VMEM((n_seq, padded, width), jnp.bfloat16),
            pltpu.VMEM(prefix.shape, jnp.bfloat16),
            pltpu.VMEM((n_dom * local, rows_suffix, width), jnp.bfloat16),
            pltpu.VMEM((local * rows_suffix, width), jnp.bfloat16),
            pltpu.VMEM((group * padded, prefix.shape[0]), jnp.float32),
            pltpu.VMEM((n_seq * padded, rank), jnp.float32),
            pltpu.VMEM((2, n_seq * padded, 128), jnp.float32),
            pltpu.VMEM((n_seq, padded, rank), jnp.bfloat16),
            pltpu.VMEM((n_seq, 8, padded), jnp.float32),
            pltpu.VMEM((n_seq, padded, rank), jnp.bfloat16),
            pltpu.VMEM((n_seq, 8, padded), jnp.float32),
            pltpu.SemaphoreType.DMA,
            pltpu.SemaphoreType.DMA((n_seq,)),
            pltpu.SemaphoreType.DMA((n_seq,)),
            pltpu.SemaphoreType.DMA((2, n_dom)),
            pltpu.SemaphoreType.DMA((2, n_dom)),
            pltpu.SemaphoreType.DMA((n_seq,)),
            pltpu.SemaphoreType.DMA((n_seq,)),
            pltpu.SemaphoreType.DMA((n_seq,)),
            pltpu.SemaphoreType.DMA((n_seq,)),
        ],
        compiler_params=pltpu.CompilerParams(
            collective_id=0, has_side_effects=True, vmem_limit_bytes=56 * 1024 * 1024
        ),
        name="resample_attention",
    )(ancestors, lengths, own, prefix, private_caches, new_latent)
    latent = latent.reshape(local, padded // local, rank)[:, :own_heads]
    head_values = jnp.einsum(
        "phc,hcv->phv", latent, w_uv, preferred_element_type=jnp.float32
    ).astype(jnp.bfloat16)
    return (head_values, new_caches)


def solution(mesh):
    placed = (
        P(("group", "dom"), "seq", None),
        P(("group", "dom"), "seq", None),
        P("seq", None, None),
        P("seq", None, None),
        P(("group", "seq"), None),
        P(("group", "dom"), "seq", None),
        P(("group", "dom"), None),
        P(("group", "dom")),
        P("group"),
    )
    return jax.shard_map(
        functools.partial(on_device, mesh.shape["seq"], mesh.shape["dom"]),
        mesh=mesh,
        in_specs=placed,
        out_specs=(P(("group", "dom"), "seq", None), P(("group", "dom"), "seq", None)),
        check_vma=False,
    )
```

time: 101 us -> 55 us (0.54)
  Pallas kernels: 0 us -> 38.9 us
  waiting for transfers between devices: 29.2 us -> 0 us
  blocking collectives: 19.9 us -> 0 us
  between operations: 14.2 us -> 0.68 us
  matrix products: 16.1 us -> 4.44 us
  other arithmetic: 11 us -> 0.09 us
    pallas_call x0 -> x1, Pallas kernels: none -> 38.9 us  [on_device(): pl.pallas_call(functools.partial(attention_kernel, n_seq, n_dom, scale),...]
    all_gather x2 -> x0, waiting for transfers between devices: 28.5 us -> none  [the longest x1 17.4 us: joined(): gathered = jax.tree.map(lambda a: lax.all_gather(a, axis), part)]
    all_gather x3 -> x0, blocking collectives: 19.9 us -> none  [the longest x2 10.5 us: joined(): gathered = jax.tree.map(lambda a: lax.all_gather(a, axis), part)]
    dot_general x6 -> x1, matrix products: 13.3 us -> 1.6 us  [on_device(): jnp.einsum('phc,hcv->phv', latent, w_uv, preferred_element_type=jnp.float32)]
    reduce_sum x3 -> x0, other arithmetic: 5.18 us -> none  [the longest x1 4.88 us: on_device(): prefix_sum = jnp.sum(prefix_weights, axis=1)]
    unnamed x16 -> x10, local copies, waits for them, and re-layouts: 4.67 us -> 9.8 us
    add x8 -> x0, other arithmetic: 4.66 us -> none  [the longest x3 4.56 us: merge_partials(): left_acc * left_factor[..., None] + right_acc * right_factor[..., None]]
    reshape x2 -> x0, local copies, waits for them, and re-layouts: 3.03 us -> none  [the longest x1 2.68 us: on_device(): portion.reshape(amount, -1)]
  transfers between devices with their start and end apart: 2 -> 0, of which waited for: 2 -> 0; matrix products, arithmetic and copies ran while one was open for 19% -> 0% of each run, Pallas kernels for 0% -> 0%
where the time goes in v1:
time: 55 us; the launch traced here: 54.6 us
  Pallas kernels  38.9 us (71%)
  local copies, waits for them, and re-layouts  10.5 us (19%)
  matrix products  4.44 us (8%)
  between operations  0.68 us (1%)
    pallas_call x1, Pallas kernels, on_device(): pl.pallas_call(functools.partial(attention_kernel, n_seq, n_dom, scale),...  38.9 us
    unnamed x10, local copies, waits for them, and re-layouts  9.8 us
    dot_general x1, matrix products, on_device(): jnp.einsum('phn,hnc->phc', q_nope, w_uk, preferred_element_type=jnp.float32)  2.84 us
    dot_general x1, matrix products, on_device(): jnp.einsum('phc,hcv->phv', latent, w_uv, preferred_element_type=jnp.float32)  1.6 us

profile of v1, /device:TPU:0, one launch (start us, length us, event | category | flops | bytes accessed | tf_op | source)
XLA Modules:
  0.0 54.6 jit_solution(17260402842061701969)
XLA Ops:
  0.6 0.0 copy-start
  0.6 0.8 %copy.12 = bf16[4,32,64]{2,0,1:T(4,128)(2,1)S(1)} copy(bf16[4,32,64]{2,1,0:T(8,128)(2,1)} %param.10) | data formatting | bytes 32768 | tf_op args[1]
  1.4 0.0 copy-done
  1.4 2.8 %fusion = bf16[4,32,512]{2,0,1:T(4,128)(2,1)S(1)} fusion(bf16[32,128,512]{2,1,0:T(8,128)(2,1)} %param.11, bf16[4,32,128]{2,1,0:T(8,128)(2,1)S(1)} %copy-done), kind=kOutput, calls=%fused_computation.1 | convolution fusion | flops 16842752 | bytes 4358144 | tf_op jit(solution)/shard_map/phn,hnc->phc/dot_general | solution.py:266
  4.3 0.1 pad_maximum_fusion
  4.4 0.7 %copy.13 = bf16[4,32,576]{2,1,0:T(8,128)(2,1)} copy(bf16[4,32,576]{2,0,1:T(4,128)(2,1)S(1)} %pad_maximum_fusion) | data formatting | bytes 294912 | tf_op jit(solution)/shard_map/concatenate | solution.py:269
  5.1 7.6 %copy.14.prefix_hbm = bf16[4096,576]{1,0:T(8,128)(2,1)} copy(bf16[4096,576]{0,1:T(8,128)(2,1)} %param.13) | data formatting | bytes 9437184 | tf_op args[4]
  12.7 0.0 copy-start.1
  12.7 38.9 %resample_attention.1 = (bf16[128,512]{1,0:T(8,128)(2,1)}, bf16[4,64,576]{2,1,0:T(8,128)(2,1)}) custom-call(s32[4]{0:T(128)} %anc_ref.1, s32[16]{0:T(128)} %len_ref.1, bf16[128,576]{1,0:T(8,128)(2,1)} %bitcast.8, bf16[4096,576]{1,0:T(8,128)(2,1)} %copy.14.prefix_hbm, bf16[4,64,576]{2,1,0:T(8,128)(2,1)} %cache_ref.1, bf16[4,576]{1,0:T(4,128)(2,1)} %fresh_ref.1), custom_call_target="tpu_custom_call" | custom-call | tf_op jit(solution)/shard_map/resample_attention/pallas_call | solution.py:277
  51.6 0.0 copy-start.2
  51.6 0.0 copy-done.1
  51.6 1.6 %fusion.1 = bf16[4,32,128]{2,0,1:T(4,128)(2,1)S(1)} fusion(bf16[32,512,128]{2,1,0:T(8,128)(2,1)S(1)} %copy-done.1, bf16[4,32,512]{2,1,0:T(8,128)(2,1)} %bitcast.9), kind=kOutput, calls=%fused_computation.3 | convolution fusion | flops 16793600 | bytes 4358144 | tf_op jit(solution)/shard_map/phc,hcv->phv/dot_general | solution.py:313
  53.2 0.6 %copy.16 = bf16[4,32,128]{2,1,0:T(8,128)(2,1)} copy(bf16[4,32,128]{2,0,1:T(4,128)(2,1)S(1)} %fusion.1) | data formatting | bytes 65536
  53.8 0.0 copy-done.2
  53.8 0.7 %copy.22 = bf16[4,64,576]{2,1,0:T(8,128)(2,1)} copy(bf16[4,64,576]{2,1,0:T(8,128)(2,1)S(1)} %copy-done.2) | data formatting | bytes 589824
Async XLA Ops:
  0.6 0.8 %copy-start = (bf16[4,32,128]{2,1,0:T(8,128)(2,1)S(1)}, bf16[4,32,128]{2,1,0:T(8,128)(2,1)}, u32[]{:S(2)}) copy-start(bf16[4,32,128]{2,1,0:T(8,128)(2,1)} %param.9) | copy-start | bytes 98308
  12.7 38.9 %copy-start.1 = (bf16[32,512,128]{2,1,0:T(8,128)(2,1)S(1)}, bf16[32,512,128]{2,1,0:T(8,128)(2,1)}, u32[]{:S(2)}) copy-start(bf16[32,512,128]{2,1,0:T(8,128)(2,1)} %param.12) | copy-start | bytes 12582916
  51.6 2.3 %copy-start.2 = (bf16[4,64,576]{2,1,0:T(8,128)(2,1)S(1)}, bf16[4,64,576]{2,1,0:T(8,128)(2,1)}, u32[]{:S(2)}) copy-start(bf16[4,64,576]{2,1,0:T(8,128)(2,1)} %get-tuple-element.11) | copy-start | bytes 884740

commit v2 on v1

--- a/solution.py
+++ b/solution.py
@@ -28,11 +28,12 @@
 
 def attention_kernel(
     n_seq, n_dom, scale,
-    anc_ref, len_ref, q_ref, prefix_hbm, cache_ref, fresh_ref,
+    anc_ref, len_ref, anc_wide, nope_ref, rope_ref, w_hbm, prefix_hbm, cache_ref, fresh_ref,
     latent_ref, caches_ref,
-    queries, prefix, blocks, suffix, scores, acc, stats,
-    send_acc, send_stat, recv_acc, recv_stat,
-    load_sem, q_send, q_recv, z_send, z_recv, a_send, a_recv, s_send, s_recv,
+    q_ref, weight, queries, prefix, raw, picked, chosen, asked, asked_scalar, suffix, scores, acc,
+    stats, send_acc, send_stat, recv_acc, recv_stat,
+    load_sem, q_send, q_recv, z_send, z_recv, c_send, c_recv, n_send, n_recv, n_load,
+    a_send, a_recv, s_send, s_recv,
 ):
     me = lax.axis_index("seq")
     dom = lax.axis_index("dom")
@@ -42,10 +43,14 @@
     rows = q_ref.shape[0]
     heads = rows // local
     rank = latent_ref.shape[1]
-    keys = prefix.shape[0]
+    keys = prefix.shape[1]
+    chunks = len(raw[0])
+    thick = rows_suffix // chunks
     group = 2 if n_seq % 2 == 0 else 1
 
-    load = pltpu.make_async_copy(prefix_hbm, prefix, load_sem)
+    load_w = pltpu.make_async_copy(w_hbm, weight, load_sem.at[0])
+    load_w.start()
+    load = pltpu.make_async_copy(prefix_hbm, prefix, load_sem.at[1])
     load.start()
 
     barrier = pltpu.get_barrier_semaphore()
@@ -71,52 +76,119 @@
             device_id={"seq": partner(me, step, n_seq)},
         )
 
-    def z_copy(way, step):
-        block = dom - step if way == 0 else dom + step
-        view = blocks.at[pl.ds(block * local, local)]
-        return pltpu.make_async_remote_copy(
-            src_ref=cache_ref if step == 0 else view, dst_ref=view,
-            send_sem=z_send.at[way, step], recv_sem=z_recv.at[way, step],
-            device_id={"dom": dom + 1 if way == 0 else dom - 1},
-        )
-
-    def z_arrival(way, step):
-        block = dom - step - 1 if way == 0 else dom + step + 1
-        view = blocks.at[pl.ds(block * local, local)]
-        return pltpu.make_async_remote_copy(
-            src_ref=view, dst_ref=view,
-            send_sem=z_send.at[way, step], recv_sem=z_recv.at[way, step],
-            device_id={"dom": dom + 1 if way == 0 else dom - 1},
+    def toward(way):
+        return {"dom": dom + 1 if way == 0 else dom - 1}
+
+    def z_copy(way, step, r, arrival=False):
+        hop = step + 1 if arrival else step
+        block = dom - hop if way == 0 else dom + hop
+        view = raw[way][r].at[pl.ds(block * local, local)]
+        own = cache_ref.at[:, pl.ds(r * thick, thick)]
+        return pltpu.make_async_remote_copy(
+            src_ref=own if hop == 0 else view, dst_ref=view,
+            send_sem=z_send.at[way, step, r], recv_sem=z_recv.at[way, step, r],
+            device_id=toward(way),
+        )
+
+    def c_copy(way, r):
+        return pltpu.make_async_remote_copy(
+            src_ref=chosen[way][r], dst_ref=picked[way][r],
+            send_sem=c_send.at[way, r], recv_sem=c_recv.at[way, r],
+            device_id=toward(way),
+        )
+
+    def n_copy(way):
+        return pltpu.make_async_remote_copy(
+            src_ref=anc_wide, dst_ref=asked.at[way],
+            send_sem=n_send.at[way], recv_sem=n_recv.at[way],
+            device_id=toward(1 - way),
         )
 
     def z_sends(way, step):
         if way == 0:
-            return (dom >= step) & (dom < n_dom - 1)
-        return (dom + step < n_dom) & (dom > 0)
+            return (dom >= step) & (dom < n_dom - 2)
+        return (dom + step < n_dom) & (dom > 1)
 
     def z_receives(way, step):
         if way == 0:
-            return dom >= step + 1
-        return dom + step + 1 < n_dom
-
-    def z_stage(step):
+            return (dom >= step + 1) & (dom < n_dom - 1)
+        return (dom + step + 1 < n_dom) & (dom > 0)
+
+    def selector(way):
+        return dom == (n_dom - 2 if way == 0 else 1)
+
+    def last(way):
+        return dom == (n_dom - 1 if way == 0 else 0)
+
+    def z_stage(step, r):
         for way in (0, 1):
             if step > 0:
                 @pl.when(z_receives(way, step - 1))
                 def _():
-                    z_arrival(way, step - 1).wait_recv()
-            if step < n_dom - 1:
+                    z_copy(way, step - 1, r, arrival=True).wait_recv()
+            if step < n_dom - 2:
                 @pl.when(z_sends(way, step))
                 def _():
-                    z_copy(way, step).start()
-
-    for step in range(1, n_seq):
+                    z_copy(way, step, r).start()
+            else:
+                @pl.when(selector(way))
+                def _():
+                    if r == 0:
+                        n_copy(way).wait_recv()
+                        down = pltpu.make_async_copy(
+                            asked.at[way], asked_scalar.at[way], n_load.at[way]
+                        )
+                        down.start()
+                        down.wait()
+                    for p in range(local):
+                        want = asked_scalar[way, p, 0]
+                        mine = jnp.clip(want - dom * local, 0, local - 1)
+                        here = (want >= dom * local) & (want < (dom + 1) * local)
+                        held = cache_ref[mine, pl.ds(r * thick, thick)]
+                        came = raw[way][r][want]
+                        chosen[way][r][p] = jnp.where(here, held, came)
+                    c_copy(way, r).start()
+
+    for way in (0, 1):
+        @pl.when(last(way))
+        def _():
+            n_copy(way).start()
+    if n_dom > 2:
+        for r in range(chunks):
+            z_stage(0, r)
+    stages = [(step, r) for step in range(1 if n_dom > 2 else 0, n_dom - 1) for r in range(chunks)]
+    points = 2 * (n_seq // group)
+    share = -(-len(stages) // points)
+
+    def advance():
+        for _ in range(share):
+            if stages:
+                z_stage(*stages.pop(0))
+
+    load_w.wait()
+    head_count = weight.shape[0] // nope_ref.shape[1]
+    head_row = lax.rem(lax.broadcasted_iota(jnp.int32, nope_ref.shape, 0), heads)
+    nope = nope_ref[...].astype(jnp.float32)
+    absorbed = jnp.zeros((rows, rank), jnp.float32)
+    batch = 8 if head_count % 8 == 0 else 1
+    for low in range(0, head_count, batch):
+        wide_q = jnp.concatenate(
+            [
+                jnp.where(head_row == h, nope, 0.0).astype(jnp.bfloat16)
+                for h in range(low, low + batch)
+            ],
+            axis=1,
+        )
+        deep = nope_ref.shape[1]
+        absorbed = absorbed + jnp.dot(
+            wide_q, weight[low * deep : (low + batch) * deep], preferred_element_type=jnp.float32
+        )
+    q_ref[:, :rank] = absorbed.astype(jnp.bfloat16)
+    q_ref[:, rank:] = rope_ref[...]
+    for step in [k for k in range(2, n_seq)] + [k for k in range(1, min(2, n_seq))]:
         q_copy(step).start()
-    z_stage(0)
     queries[0] = q_ref[...]
-    blocks[pl.ds(dom * local, local)] = cache_ref[...]
     load.wait()
-    stage = 1
 
     for first in range(0, n_seq, group):
         for step in range(max(first, 1), first + group):
@@ -125,23 +197,24 @@
         flat = queries[first : first + group].reshape(wide, width)
         peak = jnp.full((wide, 128), MASKED, jnp.float32)
         for tile in range(keys // KEY_TILE):
-            part = lax.dot_general(
-                flat, prefix[tile * KEY_TILE : (tile + 1) * KEY_TILE],
-                (((1,), (1,)), ((), ())), preferred_element_type=jnp.float32,
+            part = jnp.dot(
+                flat, prefix[:, tile * KEY_TILE : (tile + 1) * KEY_TILE],
+                preferred_element_type=jnp.float32,
             ) * scale
             scores[:, tile * KEY_TILE : (tile + 1) * KEY_TILE] = part
             for lane in range(KEY_TILE // 128):
                 peak = jnp.maximum(peak, part[:, lane * 128 : (lane + 1) * 128])
         top = jnp.max(peak, axis=1, keepdims=True)
+        advance()
         mass = jnp.zeros((wide, 128), jnp.float32)
         for tile in range(keys // KEY_TILE):
             weights = jnp.exp(scores[:, tile * KEY_TILE : (tile + 1) * KEY_TILE] - top)
             for lane in range(KEY_TILE // 128):
                 mass = mass + weights[:, lane * 128 : (lane + 1) * 128]
-            update = jnp.dot(
+            update = lax.dot_general(
                 weights.astype(jnp.bfloat16),
-                prefix[tile * KEY_TILE : (tile + 1) * KEY_TILE, :rank],
-                preferred_element_type=jnp.float32,
+                prefix[:rank, tile * KEY_TILE : (tile + 1) * KEY_TILE],
+                (((1,), (1,)), ((), ())), preferred_element_type=jnp.float32,
             )
             here = pl.ds(first * rows, wide)
             if tile == 0:
@@ -151,23 +224,33 @@
         total = jnp.sum(mass, axis=1, keepdims=True)
         stats[0, pl.ds(first * rows, wide)] = jnp.broadcast_to(top, (wide, 128))
         stats[1, pl.ds(first * rows, wide)] = jnp.broadcast_to(total, (wide, 128))
-        if stage < n_dom:
-            z_stage(stage)
-            stage += 1
-    while stage < n_dom:
-        z_stage(stage)
-        stage += 1
-
-    place = me * rows_suffix + lax.broadcasted_iota(jnp.int32, (rows_suffix, width), 0)
+        advance()
+    while stages:
+        advance()
+    for way in (0, 1):
+        for r in range(chunks):
+            @pl.when(last(way))
+            def _():
+                c_copy(way, r).wait_recv()
+
+    place = me * rows_suffix + lax.broadcasted_iota(jnp.int32, (thick, width), 0)
     for p in range(local):
         source = anc_ref[p]
         length = len_ref[source]
-        moved = blocks[source]
-        suffix[p * rows_suffix : (p + 1) * rows_suffix] = moved
-        fresh = jnp.broadcast_to(fresh_ref[p : p + 1].astype(jnp.float32), (rows_suffix, width))
-        caches_ref[p] = jnp.where(place == length, fresh, moved.astype(jnp.float32)).astype(
-            caches_ref.dtype
-        )
+        fresh = jnp.broadcast_to(fresh_ref[p : p + 1].astype(jnp.float32), (thick, width))
+        mine = jnp.clip(source - dom * local, 0, local - 1)
+        for r in range(chunks):
+            held = cache_ref[mine, pl.ds(r * thick, thick)]
+            lower = jnp.where(last(0), picked[0][r][p], raw[0][r][source])
+            upper = jnp.where(last(1), picked[1][r][p], raw[1][r][source])
+            moved = jnp.where(
+                source < dom * local, lower, jnp.where(source >= (dom + 1) * local, upper, held)
+            )
+            start = p * rows_suffix + r * thick
+            suffix[start : start + thick] = moved
+            caches_ref[p, r * thick : (r + 1) * thick] = jnp.where(
+                place + r * thick == length, fresh, moved.astype(jnp.float32)
+            ).astype(caches_ref.dtype)
 
     span = local * rows_suffix
     wide = group * rows
@@ -198,10 +281,10 @@
     for first in range(n_seq - group, -1, -group):
         here = pl.ds(first * rows, wide)
         flat = queries[first : first + group].reshape(wide, width)
-        raw = lax.dot_general(
+        plain = lax.dot_general(
             flat, suffix[...], (((1,), (1,)), ((), ())), preferred_element_type=jnp.float32
         ) * scale
-        masked = jnp.where(visible, raw, MASKED)
+        masked = jnp.where(visible, plain, MASKED)
         old_top = stats[0, here][:, :1]
         top = jnp.maximum(old_top, jnp.max(masked, axis=1, keepdims=True))
         keep = jnp.exp(old_top - top)
@@ -248,10 +331,19 @@
         a_copy(step).wait_send()
         s_copy(step).wait_send()
     for way in (0, 1):
-        for step in range(n_dom - 1):
-            @pl.when(z_sends(way, step))
+        @pl.when(last(way))
+        def _():
+            n_copy(way).wait_send()
+
+        for r in range(chunks):
+            @pl.when(selector(way))
             def _():
-                z_copy(way, step).wait_send()
+                c_copy(way, r).wait_send()
+
+            for step in range(n_dom - 2):
+                @pl.when(z_sends(way, step))
+                def _():
+                    z_copy(way, step, r).wait_send()
 
 
 def on_device(
@@ -263,29 +355,42 @@
     own_heads, rank = w_uv.shape[:2]
     rows = local * own_heads
     padded = -(-rows // 128) * 128
-    query_latent = jnp.einsum(
-        "phn,hnc->phc", q_nope, w_uk, preferred_element_type=jnp.float32
-    ).astype(jnp.bfloat16)
-    own = jnp.concatenate([query_latent, q_rope], axis=2)
     if padded != rows:
-        extra = padded // local - own_heads
-        own = jnp.pad(own, ((0, 0), (0, extra), (0, 0)))
-    own = own.reshape(padded, width)
+        extra = ((0, 0), (0, padded // local - own_heads), (0, 0))
+        q_nope, q_rope = jnp.pad(q_nope, extra), jnp.pad(q_rope, extra)
+    q_nope = q_nope.reshape(padded, q_nope.shape[2])
+    q_rope = q_rope.reshape(padded, q_rope.shape[2])
+    flat_w = w_uk.reshape(-1, rank)
+    keys_first = prefix.T
+    chunks = 4 if rows_suffix % 64 == 0 else 1
+    ask_rows = -(-local // 8) * 8
+    anc_wide = jnp.broadcast_to(
+        jnp.pad(ancestors, (0, ask_rows - local))[:, None], (ask_rows, 128)
+    )
+    held = pltpu.VMEM((n_dom * local, rows_suffix // chunks, width), jnp.bfloat16)
+    some = pltpu.VMEM((local, rows_suffix // chunks, width), jnp.bfloat16)
     group = 2 if n_seq % 2 == 0 else 1
     vmem = pl.BlockSpec(memory_space=pltpu.VMEM)
     smem = pl.BlockSpec(memory_space=pltpu.SMEM)
+    whole = pl.BlockSpec(memory_space=pl.ANY)
     latent, new_caches = pl.pallas_call(
         functools.partial(attention_kernel, n_seq, n_dom, scale),
         out_shape=(
             jax.ShapeDtypeStruct((padded, rank), jnp.bfloat16),
             jax.ShapeDtypeStruct(private_caches.shape, jnp.bfloat16),
         ),
-        in_specs=[smem, smem, vmem, pl.BlockSpec(memory_space=pl.ANY), vmem, vmem],
+        in_specs=[smem, smem, vmem, vmem, vmem, whole, whole, vmem, vmem],
         out_specs=(vmem, vmem),
         scratch_shapes=[
+            pltpu.VMEM((padded, width), jnp.bfloat16),
+            pltpu.VMEM(flat_w.shape, jnp.bfloat16),
             pltpu.VMEM((n_seq, padded, width), jnp.bfloat16),
-            pltpu.VMEM(prefix.shape, jnp.bfloat16),
-            pltpu.VMEM((n_dom * local, rows_suffix, width), jnp.bfloat16),
+            pltpu.VMEM(keys_first.shape, jnp.bfloat16),
+            [[held] * chunks] * 2,
+            [[some] * chunks] * 2,
+            [[some] * chunks] * 2,
+            pltpu.VMEM((2, ask_rows, 128), jnp.int32),
+            pltpu.SMEM((2, ask_rows, 128), jnp.int32),
             pltpu.VMEM((local * rows_suffix, width), jnp.bfloat16),
             pltpu.VMEM((group * padded, prefix.shape[0]), jnp.float32),
             pltpu.VMEM((n_seq * padded, rank), jnp.float32),
@@ -294,11 +399,16 @@
             pltpu.VMEM((n_seq, 8, padded), jnp.float32),
             pltpu.VMEM((n_seq, padded, rank), jnp.bfloat16),
             pltpu.VMEM((n_seq, 8, padded), jnp.float32),
-            pltpu.SemaphoreType.DMA,
-            pltpu.SemaphoreType.DMA((n_seq,)),
-            pltpu.SemaphoreType.DMA((n_seq,)),
-            pltpu.SemaphoreType.DMA((2, n_dom)),
-            pltpu.SemaphoreType.DMA((2, n_dom)),
+            pltpu.SemaphoreType.DMA((2,)),
+            pltpu.SemaphoreType.DMA((n_seq,)),
+            pltpu.SemaphoreType.DMA((n_seq,)),
+            pltpu.SemaphoreType.DMA((2, n_dom, chunks)),
+            pltpu.SemaphoreType.DMA((2, n_dom, chunks)),
+            pltpu.SemaphoreType.DMA((2, chunks)),
+            pltpu.SemaphoreType.DMA((2, chunks)),
+            pltpu.SemaphoreType.DMA((2,)),
+            pltpu.SemaphoreType.DMA((2,)),
+            pltpu.SemaphoreType.DMA((2,)),
             pltpu.SemaphoreType.DMA((n_seq,)),
             pltpu.SemaphoreType.DMA((n_seq,)),
             pltpu.SemaphoreType.DMA((n_seq,)),
@@ -308,7 +418,9 @@
             collective_id=0, has_side_effects=True, vmem_limit_bytes=56 * 1024 * 1024
         ),
         name="resample_attention",
-    )(ancestors, lengths, own, prefix, private_caches, new_latent)
+    )(
+        ancestors, lengths, anc_wide, q_nope, q_rope, flat_w, keys_first, private_caches, new_latent
+    )
     latent = latent.reshape(local, padded // local, rank)[:, :own_heads]
     head_values = jnp.einsum(
         "phc,hcv->phv", latent, w_uv, preferred_element_type=jnp.float32

time: 55 us -> 41.3 us (0.75)
  local copies, waits for them, and re-layouts: 10.5 us -> 2.69 us
  matrix products: 4.44 us -> 1.6 us
  Pallas kernels: 38.9 us -> 36.2 us
    unnamed x10 -> x6, local copies, waits for them, and re-layouts: 9.8 us -> 1.36 us
    dot_general x1 -> x0, matrix products: 2.84 us -> none  [on_device(): jnp.einsum('phn,hnc->phc', q_nope, w_uk, preferred_element_type=jnp.float32)]
    pallas_call x1, Pallas kernels: 38.9 us -> 36.2 us  [on_device(): pl.pallas_call(functools.partial(attention_kernel, n_seq, n_dom, scale),...]
    concatenate x1 -> x0, local copies, waits for them, and re-layouts: 0.69 us -> none  [on_device(): own = jnp.concatenate([query_latent, q_rope], axis=2)]
    broadcast_in_dim x0 -> x1, local copies, waits for them, and re-layouts: none -> 0.66 us  [on_device(): jnp.broadcast_to(jnp.pad(ancestors, (0, ask_rows - local))[:, None], (ask...]
    pad x0 -> x1, local copies, waits for them, and re-layouts: none -> 0.66 us  [on_device(): jnp.pad(ancestors, (0, ask_rows - local))[:, None]]
where the time goes in v2:
time: 41.3 us; the launch traced here: 41.2 us
  Pallas kernels  36.2 us (88%)
  local copies, waits for them, and re-layouts  2.69 us (7%)
  matrix products  1.6 us (4%)
  between operations  0.66 us (2%)
    pallas_call x1, Pallas kernels, on_device(): pl.pallas_call(functools.partial(attention_kernel, n_seq, n_dom, scale),...  36.2 us
    dot_general x1, matrix products, on_device(): jnp.einsum('phc,hcv->phv', latent, w_uv, preferred_element_type=jnp.float32)  1.6 us
    unnamed x6, local copies, waits for them, and re-layouts  1.36 us

profile of v2, /device:TPU:0, one launch (start us, length us, event | category | flops | bytes accessed | tf_op | source)
XLA Modules:
  0.0 41.2 jit_solution(12919530623478202268)
XLA Ops:
  0.6 0.7 %pad.4 = s32[8]{0:T(128)S(1)} pad(s32[4]{0:T(128)} %anc_ref.1, s32[]{:T(128)} %constant.0.clone.1), padding=0_4 | pad | bytes 52 | tf_op jit(solution)/shard_map/jit(_pad)/pad | solution.py:368
  1.3 0.7 %broadcast_in_dim.2.anc_wide = s32[8,128]{1,0:T(8,128)} broadcast(s32[8]{0:T(128)S(1)} %pad.4), dimensions={0} | broadcast | bytes 4128 | tf_op jit(solution)/shard_map/broadcast_in_dim | solution.py:367
  2.0 0.0 copy-start
  2.0 36.2 %resample_attention.1 = (bf16[128,512]{1,0:T(8,128)(2,1)}, bf16[4,64,576]{2,1,0:T(8,128)(2,1)}) custom-call(s32[4]{0:T(128)} %anc_ref.1, s32[16]{0:T(128)} %len_ref.1, s32[8,128]{1,0:T(8,128)} %broadcast_in_dim.2.anc_wide, bf16[128,128]{1,0:T(8,128)(2,1)} %bitcast.11, bf16[128,64]{1,0:T(8,128)(2,1)} %bitcast.12, bf16[4096,512]{1,0:T(8,128)(2,1)} %bitcast.9, ...), custom_call_target="tpu_custom_call" | custom-call | tf_op jit(solution)/shard_map/resample_attention/pallas_call | solution.py:376
  38.2 0.0 copy-start.1
  38.2 0.0 copy-done
  38.2 1.6 %fusion = bf16[4,32,128]{2,0,1:T(4,128)(2,1)S(1)} fusion(bf16[32,512,128]{2,1,0:T(8,128)(2,1)S(1)} %copy-done, bf16[4,32,512]{2,1,0:T(8,128)(2,1)} %bitcast.10), kind=kOutput, calls=%fused_computation.1 | convolution fusion | flops 16793600 | bytes 4358144 | tf_op jit(solution)/shard_map/phc,hcv->phv/dot_general | solution.py:425
  39.8 0.6 %copy.12 = bf16[4,32,128]{2,1,0:T(8,128)(2,1)} copy(bf16[4,32,128]{2,0,1:T(4,128)(2,1)S(1)} %fusion) | data formatting | bytes 65536
  40.5 0.0 copy-done.1
  40.5 0.7 %copy.16 = bf16[4,64,576]{2,1,0:T(8,128)(2,1)} copy(bf16[4,64,576]{2,1,0:T(8,128)(2,1)S(1)} %copy-done.1) | data formatting | bytes 589824
Async XLA Ops:
  2.0 36.3 %copy-start = (bf16[32,512,128]{2,1,0:T(8,128)(2,1)S(1)}, bf16[32,512,128]{2,1,0:T(8,128)(2,1)}, u32[]{:S(2)}) copy-start(bf16[32,512,128]{2,1,0:T(8,128)(2,1)} %param.12) | copy-start | bytes 12582916
  38.2 2.3 %copy-start.1 = (bf16[4,64,576]{2,1,0:T(8,128)(2,1)S(1)}, bf16[4,64,576]{2,1,0:T(8,128)(2,1)}, u32[]{:S(2)}) copy-start(bf16[4,64,576]{2,1,0:T(8,128)(2,1)} %get-tuple-element.11) | copy-start | bytes 884740
